TPU v7x, 8 devices: a whole 2x2x1 slice. The times are simulated.
8 devices in a mesh: terms: 8 (over z, y, x, core).
Axes of the slice: x: 2, y: 2, z: 1, core: 2. Of those that a mesh axis runs over, the one named last changes fastest.
Arguments:
- psi: float32 [640, 4, 4, 640], replicated
- left_env: bfloat16 [48, 640, 640], P('terms')
- two_site: bfloat16 [48, 16, 16], P('terms')
- right_env: bfloat16 [48, 640, 640], P('terms')
Outputs:
- output 1: float32 [7, 640, 4, 4, 640], replicated
- output 2: float32 [6], replicated
- output 3: float32 [6], replicated
All inputs are finite; a program needn't handle non-finite values.
Results may differ from a plain program's by a relative error of at most 0.0133512.
Values are sent between devices in bfloat16 or wider.
A program may use at most 1 GiB of HBM per device.

v0:
```python
import jax
import jax.numpy as jnp
from jax import lax
from jax.sharding import PartitionSpec as P

LANCZOS_STEPS = 6


def solution(mesh):
    groups = mesh.shape["terms"]

    def local_sigma(vec_bf, left_loc, site_loc, right_loc):
        bond = vec_bf.shape[0]
        pair = site_loc.shape[1]
        vec_flat = vec_bf.reshape(bond * pair, bond)

        def one_term(acc_sum, term):
            left_k, site_k, right_k = term
            right_out = lax.dot_general(vec_flat, right_k, (((1,), (1,)), ((), ())), preferred_element_type=jnp.float32).astype(jnp.bfloat16)
            site_out = jnp.einsum("qp,xpb->xqb", site_k, right_out.reshape(bond, pair, bond), preferred_element_type=jnp.float32).astype(jnp.bfloat16)
            return acc_sum + jnp.dot(left_k, site_out.reshape(bond, pair * bond), preferred_element_type=jnp.float32), None

        init_acc = jnp.zeros((bond, pair * bond), jnp.float32)
        return lax.scan(one_term, init_acc, (left_loc, site_loc, right_loc))[0]

    def body(psi, left_loc, site_loc, right_loc):
        bond = psi.shape[0]
        slab = bond // groups
        row_start = lax.axis_index("terms") * slab
        cur_full = psi / jnp.sqrt(jnp.sum(psi * psi))
        cur_slab = lax.dynamic_slice_in_dim(cur_full, row_start, slab, axis=0)
        prev_slab = jnp.zeros_like(cur_slab)
        beta_prev = 0.0
        vectors = [cur_full]
        alphas = []
        betas = []
        for step_idx in range(LANCZOS_STEPS):
            part_sum = local_sigma(cur_full.astype(jnp.bfloat16), left_loc, site_loc, right_loc)
            sigma_slab = lax.psum_scatter(part_sum, "terms", scatter_dimension=0, tiled=True).reshape(cur_slab.shape)
            alpha = lax.psum(jnp.sum(sigma_slab * cur_slab), "terms")
            residual = sigma_slab - alpha * cur_slab - beta_prev * prev_slab
            beta = jnp.sqrt(lax.psum(jnp.sum(residual * residual), "terms"))
            prev_slab = cur_slab
            cur_slab = residual / beta
            cur_full = lax.all_gather(cur_slab, "terms", axis=0, tiled=True)
            vectors.append(cur_full)
            alphas.append(alpha)
            betas.append(beta)
            beta_prev = beta
        return jnp.stack(vectors), jnp.stack(alphas), jnp.stack(betas)

    return jax.shard_map(body, mesh=mesh, in_specs=(P(), P("terms"), P("terms"), P("terms")), out_specs=(P(), P(), P()), check_vma=False)
```

profile of v0, /device:TPU:0, one launch (start us, length us, event | category | flops | bytes accessed | tf_op | source)
XLA Modules:
  0.0 5412.6 jit_solution(645239145773297481)
XLA Ops:
  67.7 514.5 %while.66 = (s32[]{:T(128)}, f32[640,10240]{1,0:T(8,128)}, bf16[6,640,640]{2,1,0:T(8,128)(2,1)}, bf16[6,640,640]{2,1,0:T(8,128)(2,1)}, bf16[10240,640]{1,0:T(8,1...) while((s32[]{:T(128)}, f32[640,10240]{1,0:T(8,128)}, ...), condition=%wide.region_2.3_spmd.clone, body=%wide.region_1.2_spmd.clone.sunk | while | flops 17013145600 | bytes 172036224 | solution.py:24
  205.6 27.9 select_add_fusion.12
  380.0 27.9 select_add_fusion.12
  554.3 27.9 select_add_fusion.12
  582.3 154.1 %reduce-scatter.7.cloned.1.call-done = f32[80,10240]{1,0:T(8,128)} async-done(((f32[640,10240]{1,0:T(8,128)}), f32[80,10240]{1,0:T(8,128)}) %reduce-scatter.7.cloned.1.call-update) | async-done | bytes 3276816 | tf_op jit(solution)/shard_map/reduce_scatter | solution.py:39
  802.1 125.2 %all-gather.7.cloned.1.call-done = f32[640,4,4,640]{3,2,1,0:T(4,128)} async-done(((f32[80,4,4,640]{3,2,1,0:T(4,128)}), f32[640,4,4,640]{3,2,1,0:T(4,128)}) %all-gather.7.cloned.1.call-update) | async-done | bytes 26214416 | tf_op jit(solution)/shard_map/all_gather | solution.py:45
  962.2 513.9 %while.67 = (s32[]{:T(128)}, f32[640,10240]{1,0:T(8,128)}, bf16[6,640,640]{2,1,0:T(8,128)(2,1)}, bf16[6,640,640]{2,1,0:T(8,128)(2,1)}, bf16[10240,640]{1,0:T(8,1...) while((s32[]{:T(128)}, f32[640,10240]{1,0:T(8,128)}, ...), condition=%wide.region_9.10_spmd.clone, body=%wide.region_8.9_spmd.clone.sunk | while | flops 17013145600 | bytes 172036224 | solution.py:24
  1100.2 27.9 select_add_fusion.13
  1187.2 27.9 select_add_fusion.13
  1476.2 151.3 %reduce-scatter.9.cloned.1.call-done = f32[80,10240]{1,0:T(8,128)} async-done(((f32[640,10240]{1,0:T(8,128)}), f32[80,10240]{1,0:T(8,128)}) %reduce-scatter.9.cloned.1.call-update) | async-done | bytes 3276816 | tf_op jit(solution)/shard_map/reduce_scatter | solution.py:39
  1693.4 125.2 %all-gather.9.cloned.1.call-done = f32[640,4,4,640]{3,2,1,0:T(4,128)} async-done(((f32[80,4,4,640]{3,2,1,0:T(4,128)}), f32[640,4,4,640]{3,2,1,0:T(4,128)}) %all-gather.9.cloned.1.call-update) | async-done | bytes 26214416 | tf_op jit(solution)/shard_map/all_gather | solution.py:45
  1853.6 514.2 %while.68 = (s32[]{:T(128)}, f32[640,10240]{1,0:T(8,128)}, bf16[6,640,640]{2,1,0:T(8,128)(2,1)}, bf16[6,640,640]{2,1,0:T(8,128)(2,1)}, bf16[10240,640]{1,0:T(8,1...) while((s32[]{:T(128)}, f32[640,10240]{1,0:T(8,128)}, ...), condition=%wide.region_16.17_spmd.clone, body=%wide.region_15.16_spmd.clone.sunk | while | flops 17013145600 | bytes 172036224 | solution.py:24
  1991.7 27.9 select_add_fusion.14
  2078.7 27.9 select_add_fusion.14
  2252.8 27.9 select_add_fusion.14
  2339.9 27.9 select_add_fusion.14
  2367.8 151.3 %reduce-scatter.11.cloned.1.call-done = f32[80,10240]{1,0:T(8,128)} async-done(((f32[640,10240]{1,0:T(8,128)}), f32[80,10240]{1,0:T(8,128)}) %reduce-scatter.11.cloned.1.call-update) | async-done | bytes 3276816 | tf_op jit(solution)/shard_map/reduce_scatter | solution.py:39
  2586.0 125.2 %all-gather.11.cloned.1.call-done = f32[640,4,4,640]{3,2,1,0:T(4,128)} async-done(((f32[80,4,4,640]{3,2,1,0:T(4,128)}), f32[640,4,4,640]{3,2,1,0:T(4,128)}) %all-gather.11.cloned.1.call-update) | async-done | bytes 26214416 | tf_op jit(solution)/shard_map/all_gather | solution.py:45
  2746.2 513.9 %while.69 = (s32[]{:T(128)}, f32[640,10240]{1,0:T(8,128)}, bf16[6,640,640]{2,1,0:T(8,128)(2,1)}, bf16[6,640,640]{2,1,0:T(8,128)(2,1)}, bf16[10240,640]{1,0:T(8,1...) while((s32[]{:T(128)}, f32[640,10240]{1,0:T(8,128)}, ...), condition=%wide.region_23.24_spmd.clone, body=%wide.region_22.23_spmd.clone.sunk | while | flops 17013145600 | bytes 172036224 | solution.py:24
  2883.9 27.9 select_add_fusion.15
  3058.0 27.9 select_add_fusion.15
  3145.1 27.9 select_add_fusion.15
  3232.2 27.9 select_add_fusion.15
  3260.1 151.2 %reduce-scatter.13.cloned.1.call-done = f32[80,10240]{1,0:T(8,128)} async-done(((f32[640,10240]{1,0:T(8,128)}), f32[80,10240]{1,0:T(8,128)}) %reduce-scatter.13.cloned.1.call-update) | async-done | bytes 3276816 | tf_op jit(solution)/shard_map/reduce_scatter | solution.py:39
  3476.7 125.2 %all-gather.13.cloned.1.call-done = f32[640,4,4,640]{3,2,1,0:T(4,128)} async-done(((f32[80,4,4,640]{3,2,1,0:T(4,128)}), f32[640,4,4,640]{3,2,1,0:T(4,128)}) %all-gather.13.cloned.1.call-update) | async-done | bytes 26214416 | tf_op jit(solution)/shard_map/all_gather | solution.py:45
  3636.9 513.9 %while.70 = (s32[]{:T(128)}, f32[640,10240]{1,0:T(8,128)}, bf16[6,640,640]{2,1,0:T(8,128)(2,1)}, bf16[6,640,640]{2,1,0:T(8,128)(2,1)}, bf16[10240,640]{1,0:T(8,1...) while((s32[]{:T(128)}, f32[640,10240]{1,0:T(8,128)}, ...), condition=%wide.region_30.31_spmd.clone, body=%wide.region_29.30_spmd.clone.sunk | while | flops 17013145600 | bytes 172036224 | solution.py:24
  3948.8 27.9 select_add_fusion.16
  4150.9 151.2 %reduce-scatter.15.cloned.1.call-done = f32[80,10240]{1,0:T(8,128)} async-done(((f32[640,10240]{1,0:T(8,128)}), f32[80,10240]{1,0:T(8,128)}) %reduce-scatter.15.cloned.1.call-update) | async-done | bytes 3276816 | tf_op jit(solution)/shard_map/reduce_scatter | solution.py:39
  4369.5 125.2 %all-gather.15.cloned.1.call-done = f32[640,4,4,640]{3,2,1,0:T(4,128)} async-done(((f32[80,4,4,640]{3,2,1,0:T(4,128)}), f32[640,4,4,640]{3,2,1,0:T(4,128)}) %all-gather.15.cloned.1.call-update) | async-done | bytes 26214416 | tf_op jit(solution)/shard_map/all_gather | solution.py:45
  4529.7 512.9 %while.71 = (s32[]{:T(128)}, f32[640,10240]{1,0:T(8,128)}, bf16[6,640,640]{2,1,0:T(8,128)(2,1)}, bf16[6,640,640]{2,1,0:T(8,128)(2,1)}, bf16[10240,640]{1,0:T(8,1...) while((s32[]{:T(128)}, f32[640,10240]{1,0:T(8,128)}, ...), condition=%wide.region_37.38_spmd.clone, body=%wide.region_36.37_spmd.clone.sunk | while | flops 17013145600 | bytes 172036224 | solution.py:24
  5014.7 27.9 select_add_fusion.17
  5042.6 151.2 %reduce-scatter.17.cloned.1.call-done = f32[80,10240]{1,0:T(8,128)} async-done(((f32[640,10240]{1,0:T(8,128)}), f32[80,10240]{1,0:T(8,128)}) %reduce-scatter.17.cloned.1.call-update) | async-done | bytes 3276816 | tf_op jit(solution)/shard_map/reduce_scatter | solution.py:39
  (270 shorter events, 3438.2 us)
Async XLA Ops:
  7.2 729.2 %reduce-scatter.7.cloned.1.call-start = ((), (), s32[]{:S(2)}) async-start(), calls=%async_computation.6 | async-start | bytes 29491200 | tf_op jit(solution)/shard_map/reduce_scatter | solution.py:39
  582.2 345.0 %all-gather.7.cloned.1.call-start = ((), (), s32[]{:S(2)}) async-start(), calls=%async_computation.7 | async-start | bytes 29491200 | tf_op jit(solution)/shard_map/all_gather | solution.py:45
  802.0 825.5 %reduce-scatter.9.cloned.1.call-start = ((), (), s32[]{:S(2)}) async-start(), calls=%async_computation.8 | async-start | bytes 29491200 | tf_op jit(solution)/shard_map/reduce_scatter | solution.py:39
  1476.2 156.6 %copy-start.6 = (f32[80,4,4,640]{3,2,1,0:T(4,128)S(1)}, f32[80,4,4,640]{3,2,1,0:T(4,128)}, u32[]{:S(2)}) copy-start(f32[80,4,4,640]{3,2,1,0:T(4,128)} %broadcast_divide_fusion.6) | copy-start | bytes 9830404
  1476.2 342.4 %all-gather.9.cloned.1.call-start = ((), (), s32[]{:S(2)}) async-start(), calls=%async_computation.9 | async-start | bytes 29491200 | tf_op jit(solution)/shard_map/all_gather | solution.py:45
  1666.3 165.9 %copy-start.3 = (f32[80,4,4,640]{3,2,1,0:T(4,128)}, f32[80,4,4,640]{3,2,1,0:T(4,128)S(1)}, u32[]{:S(2)}) copy-start(f32[80,4,4,640]{3,2,1,0:T(4,128)S(1)} %get-tuple-element.408) | copy-start | bytes 9830404
  1693.3 825.8 %reduce-scatter.11.cloned.1.call-start = ((), (), s32[]{:S(2)}) async-start(), calls=%async_computation.10 | async-start | bytes 29491200 | tf_op jit(solution)/shard_map/reduce_scatter | solution.py:39
  1832.3 21.3 copy-start.7
  2367.8 156.6 %copy-start.4 = (f32[80,4,4,640]{3,2,1,0:T(4,128)S(1)}, f32[80,4,4,640]{3,2,1,0:T(4,128)}, u32[]{:S(2)}) copy-start(f32[80,4,4,640]{3,2,1,0:T(4,128)} %copy-done.3) | copy-start | bytes 9830404
  2367.8 343.4 %all-gather.11.cloned.1.call-start = ((), (), s32[]{:S(2)}) async-start(), calls=%async_computation.11 | async-start | bytes 29491200 | tf_op jit(solution)/shard_map/all_gather | solution.py:45
  2586.0 825.4 %reduce-scatter.13.cloned.1.call-start = ((), (), s32[]{:S(2)}) async-start(), calls=%async_computation.12 | async-start | bytes 29491200 | tf_op jit(solution)/shard_map/reduce_scatter | solution.py:39
  3260.1 156.8 %copy-start.5 = (f32[80,4,4,640]{3,2,1,0:T(4,128)S(1)}, f32[80,4,4,640]{3,2,1,0:T(4,128)}, u32[]{:S(2)}) copy-start(f32[80,4,4,640]{3,2,1,0:T(4,128)} %get-tuple-element.406) | copy-start | bytes 9830404
  3260.1 341.8 %all-gather.13.cloned.1.call-start = ((), (), s32[]{:S(2)}) async-start(), calls=%async_computation.13 | async-start | bytes 29491200 | tf_op jit(solution)/shard_map/all_gather | solution.py:45
  3449.5 166.1 %copy-start = (f32[80,4,4,640]{3,2,1,0:T(4,128)}, f32[80,4,4,640]{3,2,1,0:T(4,128)S(1)}, u32[]{:S(2)}) copy-start(f32[80,4,4,640]{3,2,1,0:T(4,128)S(1)} %get-tuple-element.404) | copy-start | bytes 9830404
  3476.6 825.5 %reduce-scatter.15.cloned.1.call-start = ((), (), s32[]{:S(2)}) async-start(), calls=%async_computation.14 | async-start | bytes 29491200 | tf_op jit(solution)/shard_map/reduce_scatter | solution.py:39
  4150.8 156.6 %copy-start.1 = (f32[80,4,4,640]{3,2,1,0:T(4,128)S(1)}, f32[80,4,4,640]{3,2,1,0:T(4,128)}, u32[]{:S(2)}) copy-start(f32[80,4,4,640]{3,2,1,0:T(4,128)} %copy-done) | copy-start | bytes 9830404
  4150.8 343.8 %all-gather.15.cloned.1.call-start = ((), (), s32[]{:S(2)}) async-start(), calls=%async_computation.15 | async-start | bytes 29491200 | tf_op jit(solution)/shard_map/all_gather | solution.py:45
  4369.4 824.4 %reduce-scatter.17.cloned.1.call-start = ((), (), s32[]{:S(2)}) async-start(), calls=%async_computation.16 | async-start | bytes 29491200 | tf_op jit(solution)/shard_map/reduce_scatter | solution.py:39
  5042.6 184.2 %copy-start.2 = (f32[80,4,4,640]{3,2,1,0:T(4,128)S(1)}, f32[80,4,4,640]{3,2,1,0:T(4,128)}, u32[]{:S(2)}) copy-start(f32[80,4,4,640]{3,2,1,0:T(4,128)} %copy-done) | copy-start | bytes 9830404
  5042.6 344.8 %all-gather.17.cloned.1.call-start = ((), (), s32[]{:S(2)}) async-start(), calls=%async_computation.17 | async-start | bytes 29491200 | tf_op jit(solution)/shard_map/all_gather | solution.py:45
Sparse Core Ops, SparseCore 0:
  582.3 153.9 reduce-scatter.6
  802.1 125.0 all-gather.6
  1476.3 151.1 reduce-scatter.8
  1693.4 125.0 all-gather.8
  2367.9 151.1 reduce-scatter.10
  2586.1 125.0 all-gather.10
  3260.2 151.1 reduce-scatter.12
  3476.7 125.0 all-gather.12
  4151.0 151.1 reduce-scatter.14
  4369.5 125.0 all-gather.14
  5042.7 151.1 reduce-scatter.16
  5262.2 125.0 all-gather.16
where the time goes:
time: 5450 us; the launch traced here: 5410 us
  matrix products  2010 us (37%)
  waiting for transfers between devices  1550 us (28%)
  local copies, waits for them, and re-layouts  1370 us (25%)
  blocking collectives  281 us (5%)
  other arithmetic  190 us (3%)
    dot_general x36, matrix products, one_term(): jnp.dot(left_k, site_out.reshape(bond, pair * bond), preferred_element_ty...  951 us
    reduce_scatter x6, waiting for transfers between devices, body(): lax.psum_scatter(part_sum, 'terms', scatter_dimension=0, tiled=True)  910 us
    all_gather x6, waiting for transfers between devices, body(): cur_full = lax.all_gather(cur_slab, 'terms', axis=0, tiled=True)  638 us
    convert_element_type x36, local copies, waits for them, and re-layouts, one_term(): lax.dot_general(vec_flat, right_k, (((1,), (1,)), ((), ())), preferred_el...  633 us
    dot_general x36, matrix products, one_term(): lax.dot_general(vec_flat, right_k, (((1,), (1,)), ((), ())), preferred_el...  589 us
    dot_general x36, matrix products, one_term(): jnp.einsum('qp,xpb->xqb', site_k, right_out.reshape(bond, pair, bond), pr...  467 us
    while x36, local copies, waits for them, and re-layouts  443 us
    psum x6, blocking collectives, body(): beta = jnp.sqrt(lax.psum(jnp.sum(residual * residual), 'terms'))  146 us
  transfers between devices with their start and end apart: 12, of which 12 were waited for; matrix products, arithmetic and copies ran while one was open for 2% of the time, Pallas kernels for 0%

commit v1 on v0

v1 whole, which is shorter than its diff:
```python
import functools

import jax
import jax.numpy as jnp
from jax import lax
from jax.experimental import pallas as pl
from jax.experimental.pallas import tpu as pltpu
from jax.sharding import PartitionSpec as P

LANCZOS_STEPS = 6
LANE = 128
SUB = 16
GROUP = 6
PIECES = (2, 3)
MESH = pl.DeviceIdType.MESH


def ham_kernel(bond, pair, slab, group, first, u_ref, r_ref, w_ref, l_ref, *rest):
    out_ref, y1, y2 = rest[-3:]
    inner = u_ref.shape[1] // (pair * LANE)
    chunks = bond // LANE
    bgroups = slab // SUB
    width = pair * LANE

    @pl.when(pl.program_id(0) == 0)
    def _():
        out_ref[...] = jnp.zeros_like(out_ref) if first else rest[0][...]

    def right(i, _):
        cols = pl.ds(pl.multiple_of(i * width, width), width)
        y1[:, cols] = jnp.dot(r_ref[...], u_ref[:, cols], preferred_element_type=jnp.float32).astype(jnp.bfloat16)
        return 0

    lax.fori_loop(0, inner, right, 0, unroll=True)

    blocks = [(bg, ac) for bg in range(bgroups) for ac in range(inner)]

    def site(k, _):
        w_k = w_ref[k]
        base = k * slab
        for start in range(0, len(blocks), 4):
            part = blocks[start : start + 4]
            tiles = []
            for bg, ac in part:
                sub = pl.ds(pl.multiple_of(base + bg * SUB, SUB), SUB)
                tiles.append(jnp.concatenate([y1[sub, (ac * pair + p) * LANE : (ac * pair + p + 1) * LANE] for p in range(pair)], axis=0))
            rhs = tiles[0] if len(tiles) == 1 else jnp.concatenate(tiles, axis=1)
            res = jnp.dot(w_k, rhs, preferred_element_type=jnp.float32).astype(jnp.bfloat16)
            for n, (bg, ac) in enumerate(part):
                cols = pl.ds(pl.multiple_of((k * inner + ac) * LANE, LANE), LANE)
                for q in range(pair):
                    y2[q * slab + bg * SUB : q * slab + (bg + 1) * SUB, cols] = res[q * SUB : (q + 1) * SUB, n * LANE : (n + 1) * LANE]
        return 0

    lax.fori_loop(0, group, site, 0, unroll=True)

    qs = pair // 2

    def left(i, _):
        sub = pl.ds(pl.multiple_of(i * (qs * slab), qs * slab), qs * slab)
        res = jnp.dot(y2[sub, :], l_ref[...], preferred_element_type=jnp.float32)
        for ac in range(chunks):
            for n in range(qs):
                cols = pl.ds(pl.multiple_of((ac * pair + n) * LANE + i * (qs * LANE), LANE), LANE)
                out_ref[:, cols] += res[n * slab : (n + 1) * slab, ac * LANE : (ac + 1) * LANE]
        return 0

    lax.fori_loop(0, pair // qs, left, 0, unroll=True)


def apply_ham(u_part, right_rows, site_kron, left_rows, sigma, pair, slab):
    bond = u_part.shape[0]
    terms = site_kron.shape[0]
    side = pair * SUB
    span = u_part.shape[1] // pair
    full = lambda i: (0, 0)
    flops = 2 * terms * slab * (bond * span * pair * 2 + side * side * span // SUB)
    once = pl.BlockSpec((slab, bond * pair), full, pipeline_mode=pl.Buffered(1))
    first = sigma is None
    return pl.pallas_call(
        functools.partial(ham_kernel, bond, pair, slab, GROUP, first),
        grid=(terms // GROUP,),
        in_specs=[
            pl.BlockSpec((bond, span * pair), full, pipeline_mode=pl.Buffered(1)),
            pl.BlockSpec((GROUP * slab, bond), lambda i: (i, 0)),
            pl.BlockSpec((GROUP, side, side), lambda i: (i, 0, 0)),
            pl.BlockSpec((GROUP * span, bond), lambda i: (i, 0)),
        ] + ([] if first else [once]),
        out_specs=once,
        out_shape=jax.ShapeDtypeStruct((slab, bond * pair), jnp.float32),
        scratch_shapes=[
            pltpu.VMEM((GROUP * slab, span * pair), jnp.bfloat16),
            pltpu.VMEM((pair * slab, GROUP * span), jnp.bfloat16),
        ],
        compiler_params=pltpu.CompilerParams(dimension_semantics=("arbitrary",), vmem_limit_bytes=60_000_000),
        cost_estimate=pl.CostEstimate(flops=flops, bytes_accessed=50_000_000, transcendentals=0),
        name="apply_ham",
    )(u_part, right_rows, site_kron, left_rows, *([] if first else [sigma]))


def update_kernel(devices, sig_ref, cur_ref, prev_ref, bprev_ref, nxt_ref, alpha_ref, beta_ref, *rest):
    low_refs, (parts, slots, send_sem, recv_sem) = rest[:-4], rest[-4:]
    me = lax.axis_index("terms")
    rows, cols = sig_ref.shape
    step = 512

    barrier = pltpu.get_barrier_semaphore()
    for off in range(1, devices):
        pl.semaphore_signal(barrier, inc=1, device_id=(lax.rem(me + off, devices),), device_id_type=MESH)

    def fold(val):
        return val.reshape(rows // 8, 8, step // LANE, LANE).sum(axis=(0, 2))

    def view(i):
        return pl.ds(pl.multiple_of(i * step, step), step)

    def all_sum(phase):
        slots[phase, me] = parts[phase]
        copies = []
        for off in range(1, devices):
            copies.append(pltpu.make_async_remote_copy(
                src_ref=parts.at[phase],
                dst_ref=slots.at[phase, me],
                send_sem=send_sem.at[phase, off],
                recv_sem=recv_sem.at[phase, off],
                device_id=(lax.rem(me + off, devices),),
                device_id_type=MESH,
            ))
        for copy in copies:
            copy.start()
        for copy in copies:
            copy.wait()
        total = slots[phase, 0]
        for dev in range(1, devices):
            total = total + slots[phase, dev]
        return jnp.sum(jnp.sum(total, axis=0, keepdims=True), axis=1, keepdims=True)

    zero = jnp.zeros((8, LANE), jnp.float32)

    def dot_part(i, acc):
        return acc + fold(sig_ref[:, view(i)] * cur_ref[:, view(i)])

    parts[0] = lax.fori_loop(0, cols // step, dot_part, zero)
    pl.semaphore_wait(barrier, devices - 1)
    alpha = all_sum(0)
    beta_prev = bprev_ref[0:1, 0:1]

    def residual(i, acc):
        res = sig_ref[:, view(i)] - alpha * cur_ref[:, view(i)] - beta_prev * prev_ref[:, view(i)]
        nxt_ref[:, view(i)] = res
        return acc + fold(res * res)

    parts[1] = lax.fori_loop(0, cols // step, residual, zero)
    beta = jnp.sqrt(all_sum(1))

    def scale(i, _):
        val = nxt_ref[:, view(i)] / beta
        nxt_ref[:, view(i)] = val
        return val.astype(jnp.bfloat16)

    base = 0
    for low_ref in low_refs:
        def piece(i, _, base=base, low_ref=low_ref):
            low_ref[:, view(i)] = scale(i + base, 0)
            return 0

        count = low_ref.shape[1] // step
        lax.fori_loop(0, count, piece, 0)
        base += count
    if not low_refs:
        def only(i, _):
            scale(i, 0)
            return 0

        lax.fori_loop(0, cols // step, only, 0)
    alpha_ref[...] = jnp.broadcast_to(alpha, alpha_ref.shape)
    beta_ref[...] = jnp.broadcast_to(beta, beta_ref.shape)


def update(devices, widths, sigma, cur, prev, beta_prev):
    vmem = pl.BlockSpec(memory_space=pltpu.VMEM)
    shape = sigma.shape
    return pl.pallas_call(
        functools.partial(update_kernel, devices),
        out_shape=[
            jax.ShapeDtypeStruct(shape, jnp.float32),
            jax.ShapeDtypeStruct((8, LANE), jnp.float32),
            jax.ShapeDtypeStruct((8, LANE), jnp.float32),
        ] + [jax.ShapeDtypeStruct((shape[0], width), jnp.bfloat16) for width in widths],
        in_specs=[vmem] * 4,
        out_specs=[vmem] * (3 + len(widths)),
        scratch_shapes=[
            pltpu.VMEM((2, 8, LANE), jnp.float32),
            pltpu.VMEM((2, devices, 8, LANE), jnp.float32),
            pltpu.SemaphoreType.DMA((2, devices)),
            pltpu.SemaphoreType.DMA((2, devices)),
        ],
        compiler_params=pltpu.CompilerParams(collective_id=0 if widths else 1, has_side_effects=True, vmem_limit_bytes=32_000_000),
        cost_estimate=pl.CostEstimate(flops=20_000_000, bytes_accessed=20_000_000, transcendentals=0),
        name="lanczos_update",
    )(sigma, cur, prev, beta_prev)


def out_kernel(phys, rows_ref, kry_ref, out_ref, tmp):
    pair = phys * phys
    bond = rows_ref.shape[0]
    planes = bond // LANE
    for q in range(pair):
        for j in range(planes):
            tmp[j, pl.ds(q, LANE, stride=pair), :] = rows_ref[j * LANE : (j + 1) * LANE, q * LANE : (q + 1) * LANE].T

    def put(a, _):
        for n in range(4):
            row = a * 4 + n
            for j in range(planes):
                val = tmp[j, pl.ds(pl.multiple_of(row * pair, pair), pair), :]
                for s in range(phys):
                    out_ref[0, row, s, :, j * LANE : (j + 1) * LANE] = val[s * phys : (s + 1) * phys, :]
        return 0

    lax.fori_loop(0, LANE // 4, put, 0)

def write_vector(kry, rows, index, first=0):
    phys, bond = kry.shape[2], kry.shape[4]
    pair = phys * phys
    return pl.pallas_call(
        functools.partial(out_kernel, phys),
        grid=(rows.shape[1] // (pair * LANE),),
        in_specs=[pl.BlockSpec((bond, pair * LANE), lambda i: (0, i)), pl.BlockSpec(memory_space=pl.ANY)],
        out_specs=pl.BlockSpec((1, LANE, phys, phys, bond), lambda i: (index, i + first, 0, 0, 0)),
        out_shape=jax.ShapeDtypeStruct(kry.shape, kry.dtype),
        scratch_shapes=[pltpu.VMEM((bond // LANE, LANE * pair, LANE), jnp.float32)],
        input_output_aliases={1: 0},
        compiler_params=pltpu.CompilerParams(dimension_semantics=("arbitrary",), vmem_limit_bytes=48_000_000),
        cost_estimate=pl.CostEstimate(flops=30_000_000, bytes_accessed=54_000_000, transcendentals=0),
        name="write_vector",
    )(rows, kry)


def start_kernel(phys, slab, psi_ref, norm_ref, kry_ref, low_ref, cur_ref, tmp, turned):
    pair = phys * phys
    bond = psi_ref.shape[-1]
    planes = bond // LANE
    me = lax.axis_index("terms")
    norm = norm_ref[0:1, 0:1]

    def put(a, _):
        for n in range(4):
            row = a * 4 + n
            for s in range(phys):
                val = psi_ref[row, s] / norm
                kry_ref[0, row, s] = val
                for j in range(planes):
                    tmp[j, pl.ds(row * pair + s * phys, phys), :] = val[:, j * LANE : (j + 1) * LANE]
        return 0

    lax.fori_loop(0, LANE // 4, put, 0)
    for q in range(pair):
        for j in range(planes):
            val = tmp[j, pl.ds(q, LANE, stride=pair), :].T
            turned[j * LANE : (j + 1) * LANE, q * LANE : (q + 1) * LANE] = val
            low_ref[j * LANE : (j + 1) * LANE, q * LANE : (q + 1) * LANE] = val.astype(jnp.bfloat16)
    cur_ref[...] = turned[pl.ds(pl.multiple_of(me * slab, 8), slab), :]


def start_vectors(psi, norm, count, slab):
    phys, bond = psi.shape[1], psi.shape[3]
    pair = phys * phys
    return pl.pallas_call(
        functools.partial(start_kernel, phys, slab),
        grid=(bond // LANE,),
        in_specs=[pl.BlockSpec((LANE, phys, phys, bond), lambda i: (i, 0, 0, 0)), pl.BlockSpec((1, LANE), lambda i: (0, 0))],
        out_specs=[
            pl.BlockSpec((1, LANE, phys, phys, bond), lambda i: (0, i, 0, 0, 0)),
            pl.BlockSpec((bond, pair * LANE), lambda i: (0, i)),
            pl.BlockSpec((slab, pair * LANE), lambda i: (0, i)),
        ],
        out_shape=[
            jax.ShapeDtypeStruct((count,) + psi.shape, jnp.float32),
            jax.ShapeDtypeStruct((bond, bond * pair), jnp.bfloat16),
            jax.ShapeDtypeStruct((slab, bond * pair), jnp.float32),
        ],
        scratch_shapes=[pltpu.VMEM((bond // LANE, LANE * pair, LANE), jnp.float32), pltpu.VMEM((bond, pair * LANE), jnp.float32)],
        compiler_params=pltpu.CompilerParams(dimension_semantics=("arbitrary",), vmem_limit_bytes=56_000_000),
        cost_estimate=pl.CostEstimate(flops=60_000_000, bytes_accessed=70_000_000, transcendentals=0),
        name="start_vectors",
    )(psi, norm)


def solution(mesh):
    groups = mesh.shape["terms"]

    def body(psi, left_loc, site_loc, right_loc):
        bond, phys = psi.shape[0], psi.shape[1]
        pair = phys * phys
        slab = bond // groups
        chunks = bond // LANE
        row_start = lax.axis_index("terms") * slab

        bounds = [sum(PIECES[:n]) * LANE for n in range(len(PIECES) + 1)]
        spans = list(zip(bounds[:-1], bounds[1:]))
        widths = [(hi - lo) * pair for lo, hi in spans]
        site_all = lax.all_gather(site_loc, "terms", axis=0, tiled=True)
        left_loc, site_all = lax.optimization_barrier((left_loc, site_all))
        lefts = [lax.all_gather(left_loc[:, lo:hi], "terms", axis=0, tiled=True).reshape(-1, bond) for lo, hi in spans]
        right_rows = lax.all_to_all(right_loc, "terms", 1, 0, tiled=True).reshape(-1, bond)
        eye = jnp.eye(SUB, dtype=jnp.bfloat16)
        site_kron = (site_all[:, :, None, :, None] * eye[None, None, :, None, :]).reshape(-1, pair * SUB, pair * SUB)

        norm = jnp.broadcast_to(jnp.sqrt(jnp.sum(psi * psi)), (1, LANE))
        krylov, u_full, cur = start_vectors(psi, norm, LANCZOS_STEPS + 1, slab)
        prev = jnp.zeros_like(cur)
        beta = jnp.zeros((8, LANE), jnp.float32)
        us = [u_full[:, lo * pair : hi * pair] for lo, hi in spans]
        full = None
        alphas = []
        betas = []
        for step_idx in range(LANCZOS_STEPS):
            last = step_idx == LANCZOS_STEPS - 1
            sigma = None
            for u_part, left_rows in zip(us, lefts):
                sigma = apply_ham(u_part, right_rows, site_kron, left_rows, sigma, pair, slab)
            nxt, alpha, beta, *lows = update(groups, () if last else widths, sigma, cur, prev, beta)
            late = nxt
            if full is not None:
                if last:
                    late, full = lax.optimization_barrier((late, full))
                else:
                    lows[0], full = lax.optimization_barrier((lows[0], full))
            if not last:
                us = [lax.all_gather(lows[0], "terms", axis=0, tiled=True)]
            if full is not None:
                krylov = write_vector(krylov, full, step_idx)
                if not last:
                    krylov, lows[1] = lax.optimization_barrier((krylov, lows[1]))
            if not last:
                *lows, late, us[0] = lax.optimization_barrier((*lows[1:], nxt, us[0]))
                us += [lax.all_gather(low, "terms", axis=0, tiled=True) for low in lows]
                full = lax.all_gather(late, "terms", axis=0, tiled=True)
            prev, cur = cur, nxt
            alphas.append(alpha[0, 0])
            betas.append(beta[0, 0])
        cut = 3 * pair * LANE
        head = lax.all_gather(late[:, :cut], "terms", axis=0, tiled=True)
        tail = lax.all_gather(late[:, cut:], "terms", axis=0, tiled=True)
        krylov = write_vector(krylov, head, LANCZOS_STEPS)
        krylov = write_vector(krylov, tail, LANCZOS_STEPS, cut // (pair * LANE))
        return krylov, jnp.stack(alphas), jnp.stack(betas)

    return jax.shard_map(body, mesh=mesh, in_specs=(P(), P("terms"), P("terms"), P("terms")), out_specs=(P(), P(), P()), check_vma=False)
```

time: 5450 us -> 1650 us (0.30)
  matrix products: 2010 us -> 0 us
  waiting for transfers between devices: 1550 us -> 240 us
  local copies, waits for them, and re-layouts: 1370 us -> 91.7 us
  Pallas kernels: 0 us -> 1250 us
  blocking collectives: 281 us -> 14.1 us
  other arithmetic: 190 us -> 21.9 us
    dot_general x108 -> x0, matrix products: 2010 us -> none  [the longest x36 951 us: one_term(): jnp.dot(left_k, site_out.reshape(bond, pair * bond), preferred_element_ty...]
    pallas_call x0 -> x26, Pallas kernels: none -> 1250 us  [the longest x12 978 us: apply_ham(): pl.pallas_call(functools.partial(ham_kernel, bond, pair, slab, GROUP, fir...]
    reduce_scatter x6 -> x0, waiting for transfers between devices: 910 us -> none  [body(): lax.psum_scatter(part_sum, 'terms', scatter_dimension=0, tiled=True)]
    convert_element_type x36 -> x0, local copies, waits for them, and re-layouts: 633 us -> none  [one_term(): lax.dot_general(vec_flat, right_k, (((1,), (1,)), ((), ())), preferred_el...]
    while x36 -> x0, local copies, waits for them, and re-layouts: 443 us -> none
    all_gather x6 -> x19, waiting for transfers between devices: 638 us -> 212 us  [the longest x5 79.1 us: body(): us = [lax.all_gather(lows[0], 'terms', axis=0, tiled=True)]]
    psum x12 -> x0, blocking collectives: 281 us -> none  [the longest x6 146 us: body(): beta = jnp.sqrt(lax.psum(jnp.sum(residual * residual), 'terms'))]
    reshape x12 -> x0, local copies, waits for them, and re-layouts: 158 us -> none  [the longest x6 128 us: local_sigma(): vec_flat = vec_bf.reshape(bond * pair, bond)]
  transfers between devices with their start and end apart: 12 -> 20, of which waited for: 12 -> 10; matrix products, arithmetic and copies ran while one was open for 2% -> 6% of each run, Pallas kernels for 0% -> 69%
where the time goes in v1:
time: 1650 us; the launch traced here: 1640 us
  Pallas kernels  1250 us (76%)
  waiting for transfers between devices  240 us (15%)
  local copies, waits for them, and re-layouts  91.7 us (6%)
  other arithmetic  21.9 us (1%)
    pallas_call x12, Pallas kernels, apply_ham(): pl.pallas_call(functools.partial(ham_kernel, bond, pair, slab, GROUP, fir...  978 us
    pallas_call x7, Pallas kernels, write_vector(): pl.pallas_call(functools.partial(out_kernel, phys), grid=(rows.shape[1] /...  150 us
    pallas_call x6, Pallas kernels, update(): pl.pallas_call(functools.partial(update_kernel, devices), out_shape=[jax....  91.8 us
    all_gather x5, waiting for transfers between devices, body(): us = [lax.all_gather(lows[0], 'terms', axis=0, tiled=True)]  79.1 us
    all_gather x2, waiting for transfers between devices, body(): lax.all_gather(left_loc[:, lo:hi], 'terms', axis=0, tiled=True)  52.2 us
    all_gather x1, waiting for transfers between devices, body(): tail = lax.all_gather(late[:, cut:], 'terms', axis=0, tiled=True)  42.9 us
    all_gather x1, waiting for transfers between devices, body(): head = lax.all_gather(late[:, :cut], 'terms', axis=0, tiled=True)  37.7 us
    pallas_call x1, Pallas kernels, start_vectors(): pl.pallas_call(functools.partial(start_kernel, phys, slab), grid=(bond //...  34.7 us
  transfers between devices with their start and end apart: 20, of which 10 were waited for; matrix products, arithmetic and copies ran while one was open for 6% of the time, Pallas kernels for 69%

profile of v1, /device:TPU:0, one launch (start us, length us, event | category | flops | bytes accessed | tf_op | source)
XLA Modules:
  0.0 1642.2 jit_solution(3251860249774398291)
XLA Ops:
  7.2 14.1 all_gather.60
  40.2 15.9 multiply_reduce_fusion
  56.9 34.7 %start_vectors.1 = (f32[7,640,4,4,640]{4,3,2,1,0:T(4,128)}, bf16[640,10240]{1,0:T(8,128)(2,1)}, f32[80,10240]{1,0:T(8,128)}) custom-call(f32[640,4,4,640]{3,2,1,0:T(4,128)} %psi_ref.1, f32[1,128]{1,0:T(1,128)S(1)} %broadcast_in_dim.11.norm_ref), custom_call_target="tpu_custom_call" | custom-call | flops 60000000 | bytes 70000000 | tf_op jit(solution)/shard_map/start_vectors/pallas_call | solution.py:269
  112.1 17.4 %copy.21 = bf16[48,256,256]{2,1,0:T(8,128)(2,1)} copy(bf16[48,256,256]{0,2,1:T(8,128)(2,1)} %bitcast.21) | data formatting | bytes 12582912 | tf_op jit(solution)/shard_map/mul | solution.py:308
  135.4 24.8 %all-to-all-done = bf16[6,640,640]{2,0,1:T(8,128)(2,1)} async-done(((bf16[6,640,640]{2,0,1:T(8,128)(2,1)}), bf16[6,640,640]{2,0,1:T(8,128)(2,1)}, u32[]{:S(2)}, u32[]{:S(2)}) %all-to-all-start) | async-done | bytes 4915232 | tf_op jit(solution)/shard_map/all_to_all | solution.py:306
  169.6 66.1 %apply_ham.12.rest_0_ = f32[80,10240]{1,0:T(8,128)} custom-call(bf16[640,4096]{1,0:T(8,128)(2,1)} %slice.56.u_ref, bf16[3840,640]{1,0:T(8,128)(2,1)} %bitcast.22, bf16[48,256,256]{2,1,0:T(8,128)(2,1)} %broadcast_multiply_fusion.w_ref, bf16[12288,640]{1,0:T(8,128)(2,1)} %bitcast.40), custom_call_target="tpu_custom_call" | custom-call | flops 48318382080 | bytes 50000000 | tf_op jit(solution)/shard_map/apply_ham/pallas_call | solution.py:80
  235.8 48.5 %all-gather.20.cloned.1.call-done = bf16[48,384,640]{2,1,0:T(8,128)(2,1)} async-done(((bf16[6,384,640]{2,1,0:T(8,128)(2,1)}), bf16[48,384,640]{2,1,0:T(8,128)(2,1)}) %all-gather.20.cloned.1.call-update) | async-done | bytes 23592976 | tf_op jit(solution)/shard_map/all_gather | solution.py:305
  284.3 96.9 %apply_ham.13.sig_ref = f32[80,10240]{1,0:T(8,128)} custom-call(bf16[640,6144]{1,0:T(8,128)(2,1)} %slice.54.u_ref, bf16[3840,640]{1,0:T(8,128)(2,1)} %bitcast.23, bf16[48,256,256]{2,1,0:T(8,128)(2,1)} %broadcast_multiply_fusion.w_ref, bf16[18432,640]{1,0:T(8,128)(2,1)} %bitcast.34, f32[80,10240]{1,0:T(8,128)} %apply_ham.12.rest_0_), custom_call_target="tpu_custom_call" | custom-call | flops 72477573120 | bytes 50000000 | tf_op jit(solution)/shard_map/apply_ham/pallas_call | solution.py:80
  398.3 35.3 %all-gather.24.cloned.1.call-done.u_ref = bf16[640,4096]{1,0:T(8,128)(2,1)} async-done(((bf16[80,4096]{1,0:T(8,128)(2,1)}), bf16[640,4096]{1,0:T(8,128)(2,1)}) %all-gather.24.cloned.1.call-update) | async-done | bytes 5242896 | tf_op jit(solution)/shard_map/all_gather | solution.py:331
  434.2 66.3 %apply_ham.14.rest_0_ = f32[80,10240]{1,0:T(8,128)} custom-call(bf16[640,4096]{1,0:T(8,128)(2,1)} %all-gather.24.cloned.1.call-done.u_ref, bf16[3840,640]{1,0:T(8,128)(2,1)} %bitcast.24, bf16[48,256,256]{2,1,0:T(8,128)(2,1)} %broadcast_multiply_fusion.w_ref, bf16[12288,640]{1,0:T(8,128)(2,1)} %bitcast.41), custom_call_target="tpu_custom_call" | custom-call | flops 48318382080 | bytes 50000000 | tf_op jit(solution)/shard_map/apply_ham/pallas_call | solution.py:80
  500.5 97.0 %apply_ham.15.sig_ref = f32[80,10240]{1,0:T(8,128)} custom-call(bf16[640,6144]{1,0:T(8,128)(2,1)} %all-gather.26.cloned.1.call-done.u_ref, bf16[3840,640]{1,0:T(8,128)(2,1)} %bitcast.25, bf16[48,256,256]{2,1,0:T(8,128)(2,1)} %broadcast_multiply_fusion.w_ref, bf16[18432,640]{1,0:T(8,128)(2,1)} %bitcast.35, f32[80,10240]{1,0:T(8,128)} %apply_ham.14.rest_0_), custom_call_target="tpu_custom_call" | custom-call | flops 72477573120 | bytes 50000000 | tf_op jit(solution)/shard_map/apply_ham/pallas_call | solution.py:80
  599.5 15.2 lanczos_update.7
  615.6 24.4 %write_vector.7.kry_ref = f32[7,640,4,4,640]{4,3,2,1,0:T(4,128)} custom-call(f32[640,10240]{1,0:T(8,128)} %all-gather.28.cloned.1.call-done.rows_ref, f32[7,640,4,4,640]{4,3,2,1,0:T(4,128)} %get-tuple-element.82.kry_ref), custom_call_target="tpu_custom_call", output_to_operand_aliasing={{}: (1, {})} | custom-call | flops 30000000 | bytes 54000000 | tf_op jit(solution)/shard_map/write_vector/pallas_call | solution.py:226
  651.7 66.2 %apply_ham.16.rest_0_ = f32[80,10240]{1,0:T(8,128)} custom-call(bf16[640,4096]{1,0:T(8,128)(2,1)} %all-gather.30.cloned.1.call-done.u_ref, bf16[3840,640]{1,0:T(8,128)(2,1)} %bitcast.26, bf16[48,256,256]{2,1,0:T(8,128)(2,1)} %broadcast_multiply_fusion.w_ref, bf16[12288,640]{1,0:T(8,128)(2,1)} %bitcast.42), custom_call_target="tpu_custom_call" | custom-call | flops 48318382080 | bytes 50000000 | tf_op jit(solution)/shard_map/apply_ham/pallas_call | solution.py:80
  717.9 96.6 %apply_ham.17.sig_ref = f32[80,10240]{1,0:T(8,128)} custom-call(bf16[640,6144]{1,0:T(8,128)(2,1)} %all-gather.32.cloned.1.call-done.u_ref, bf16[3840,640]{1,0:T(8,128)(2,1)} %bitcast.27, bf16[48,256,256]{2,1,0:T(8,128)(2,1)} %broadcast_multiply_fusion.w_ref, bf16[18432,640]{1,0:T(8,128)(2,1)} %bitcast.36, f32[80,10240]{1,0:T(8,128)} %apply_ham.16.rest_0_), custom_call_target="tpu_custom_call" | custom-call | flops 72477573120 | bytes 50000000 | tf_op jit(solution)/shard_map/apply_ham/pallas_call | solution.py:80
  816.4 16.5 %lanczos_update.8 = (f32[80,10240]{1,0:T(8,128)}, f32[8,128]{1,0:T(8,128)S(1)}, f32[8,128]{1,0:T(8,128)S(1)}, bf16[80,4096]{1,0:T(8,128)(2,1)}, bf16[80,6144]{1,0:T(8,128)(2,1)}) custom-call(f32[80,10240]{1,0:T(8,128)S(1)} %copy-done.4, f32[80,10240]{1,0:T(8,128)} %get-tuple-element.91.cur_ref.prev_ref, f32[80,10240]{1,0:T(8,128)} %get-tuple-element.80.cur_ref.prev_ref, ...), custom_call_target="tpu_custom_call" | custom-call | flops 20000000 | bytes 20000000 | tf_op jit(solution)/shard_map/lanczos_update/pallas_call | solution.py:183
  833.0 24.4 %write_vector.8.kry_ref = f32[7,640,4,4,640]{4,3,2,1,0:T(4,128)} custom-call(f32[640,10240]{1,0:T(8,128)} %all-gather.34.cloned.1.call-done.rows_ref, f32[7,640,4,4,640]{4,3,2,1,0:T(4,128)} %write_vector.7.kry_ref), custom_call_target="tpu_custom_call", output_to_operand_aliasing={{}: (1, {})} | custom-call | flops 30000000 | bytes 54000000 | tf_op jit(solution)/shard_map/write_vector/pallas_call | solution.py:226
  869.2 66.5 %apply_ham.18.rest_0_ = f32[80,10240]{1,0:T(8,128)} custom-call(bf16[640,4096]{1,0:T(8,128)(2,1)} %all-gather.36.cloned.1.call-done.u_ref, bf16[3840,640]{1,0:T(8,128)(2,1)} %bitcast.28, bf16[48,256,256]{2,1,0:T(8,128)(2,1)} %broadcast_multiply_fusion.w_ref, bf16[12288,640]{1,0:T(8,128)(2,1)} %bitcast.43), custom_call_target="tpu_custom_call" | custom-call | flops 48318382080 | bytes 50000000 | tf_op jit(solution)/shard_map/apply_ham/pallas_call | solution.py:80
  935.6 96.6 %apply_ham.19.sig_ref = f32[80,10240]{1,0:T(8,128)} custom-call(bf16[640,6144]{1,0:T(8,128)(2,1)} %all-gather.38.cloned.1.call-done.u_ref, bf16[3840,640]{1,0:T(8,128)(2,1)} %bitcast.29, bf16[48,256,256]{2,1,0:T(8,128)(2,1)} %broadcast_multiply_fusion.w_ref, bf16[18432,640]{1,0:T(8,128)(2,1)} %bitcast.37, f32[80,10240]{1,0:T(8,128)} %apply_ham.18.rest_0_), custom_call_target="tpu_custom_call" | custom-call | flops 72477573120 | bytes 50000000 | tf_op jit(solution)/shard_map/apply_ham/pallas_call | solution.py:80
  1034.1 16.5 %lanczos_update.9 = (f32[80,10240]{1,0:T(8,128)}, f32[8,128]{1,0:T(8,128)S(1)}, f32[8,128]{1,0:T(8,128)S(1)}, bf16[80,4096]{1,0:T(8,128)(2,1)}, bf16[80,6144]{1,0:T(8,128)(2,1)}) custom-call(f32[80,10240]{1,0:T(8,128)S(1)} %copy-done.5, f32[80,10240]{1,0:T(8,128)} %get-tuple-element.102.cur_ref.prev_ref, f32[80,10240]{1,0:T(8,128)} %get-tuple-element.91.cur_ref.prev_ref, ...), custom_call_target="tpu_custom_call" | custom-call | flops 20000000 | bytes 20000000 | tf_op jit(solution)/shard_map/lanczos_update/pallas_call | solution.py:183
  1050.7 24.4 %write_vector.9.kry_ref = f32[7,640,4,4,640]{4,3,2,1,0:T(4,128)} custom-call(f32[640,10240]{1,0:T(8,128)} %all-gather.40.cloned.1.call-done.rows_ref, f32[7,640,4,4,640]{4,3,2,1,0:T(4,128)} %write_vector.8.kry_ref), custom_call_target="tpu_custom_call", output_to_operand_aliasing={{}: (1, {})} | custom-call | flops 30000000 | bytes 54000000 | tf_op jit(solution)/shard_map/write_vector/pallas_call | solution.py:226
  1086.7 66.1 %apply_ham.20.rest_0_ = f32[80,10240]{1,0:T(8,128)} custom-call(bf16[640,4096]{1,0:T(8,128)(2,1)} %all-gather.42.cloned.1.call-done.u_ref, bf16[3840,640]{1,0:T(8,128)(2,1)} %bitcast.30, bf16[48,256,256]{2,1,0:T(8,128)(2,1)} %broadcast_multiply_fusion.w_ref, bf16[12288,640]{1,0:T(8,128)(2,1)} %bitcast.44), custom_call_target="tpu_custom_call" | custom-call | flops 48318382080 | bytes 50000000 | tf_op jit(solution)/shard_map/apply_ham/pallas_call | solution.py:80
  1152.8 96.6 %apply_ham.21.sig_ref = f32[80,10240]{1,0:T(8,128)} custom-call(bf16[640,6144]{1,0:T(8,128)(2,1)} %all-gather.44.cloned.1.call-done.u_ref, bf16[3840,640]{1,0:T(8,128)(2,1)} %bitcast.31, bf16[48,256,256]{2,1,0:T(8,128)(2,1)} %broadcast_multiply_fusion.w_ref, bf16[18432,640]{1,0:T(8,128)(2,1)} %bitcast.38, f32[80,10240]{1,0:T(8,128)} %apply_ham.20.rest_0_), custom_call_target="tpu_custom_call" | custom-call | flops 72477573120 | bytes 50000000 | tf_op jit(solution)/shard_map/apply_ham/pallas_call | solution.py:80
  1251.3 16.4 %lanczos_update.10 = (f32[80,10240]{1,0:T(8,128)}, f32[8,128]{1,0:T(8,128)S(1)}, f32[8,128]{1,0:T(8,128)S(1)}, bf16[80,4096]{1,0:T(8,128)(2,1)}, bf16[80,6144]{1,0:T(8,128)(2,1)}) custom-call(f32[80,10240]{1,0:T(8,128)S(1)} %copy-done.6, f32[80,10240]{1,0:T(8,128)} %get-tuple-element.113.cur_ref.prev_ref, f32[80,10240]{1,0:T(8,128)} %get-tuple-element.102.cur_ref.prev_ref, ...), custom_call_target="tpu_custom_call" | custom-call | flops 20000000 | bytes 20000000 | tf_op jit(solution)/shard_map/lanczos_update/pallas_call | solution.py:183
  1267.8 24.4 %write_vector.10.kry_ref = f32[7,640,4,4,640]{4,3,2,1,0:T(4,128)} custom-call(f32[640,10240]{1,0:T(8,128)} %all-gather.46.cloned.1.call-done.rows_ref, f32[7,640,4,4,640]{4,3,2,1,0:T(4,128)} %write_vector.9.kry_ref), custom_call_target="tpu_custom_call", output_to_operand_aliasing={{}: (1, {})} | custom-call | flops 30000000 | bytes 54000000 | tf_op jit(solution)/shard_map/write_vector/pallas_call | solution.py:226
  1303.8 66.4 %apply_ham.22.rest_0_ = f32[80,10240]{1,0:T(8,128)} custom-call(bf16[640,4096]{1,0:T(8,128)(2,1)} %all-gather.48.cloned.1.call-done.u_ref, bf16[3840,640]{1,0:T(8,128)(2,1)} %bitcast.32, bf16[48,256,256]{2,1,0:T(8,128)(2,1)} %broadcast_multiply_fusion.w_ref, bf16[12288,640]{1,0:T(8,128)(2,1)} %bitcast.45), custom_call_target="tpu_custom_call" | custom-call | flops 48318382080 | bytes 50000000 | tf_op jit(solution)/shard_map/apply_ham/pallas_call | solution.py:80
  1370.2 96.6 %apply_ham.23.sig_ref = f32[80,10240]{1,0:T(8,128)} custom-call(bf16[640,6144]{1,0:T(8,128)(2,1)} %all-gather.50.cloned.1.call-done.u_ref, bf16[3840,640]{1,0:T(8,128)(2,1)} %bitcast.33, bf16[48,256,256]{2,1,0:T(8,128)(2,1)} %broadcast_multiply_fusion.w_ref, bf16[18432,640]{1,0:T(8,128)(2,1)} %bitcast.39, f32[80,10240]{1,0:T(8,128)} %apply_ham.22.rest_0_), custom_call_target="tpu_custom_call" | custom-call | flops 72477573120 | bytes 50000000 | tf_op jit(solution)/shard_map/apply_ham/pallas_call | solution.py:80
  1468.7 14.1 lanczos_update.11
  1502.0 24.5 %write_vector.11.kry_ref = f32[7,640,4,4,640]{4,3,2,1,0:T(4,128)} custom-call(f32[640,10240]{1,0:T(8,128)} %all-gather.52.cloned.1.call-done.rows_ref, f32[7,640,4,4,640]{4,3,2,1,0:T(4,128)} %write_vector.10.kry_ref), custom_call_target="tpu_custom_call", output_to_operand_aliasing={{}: (1, {})} | custom-call | flops 30000000 | bytes 54000000 | tf_op jit(solution)/shard_map/write_vector/pallas_call | solution.py:226
  1526.6 37.7 %all-gather.56.cloned.1.call-done.rows_ref = f32[640,6144]{1,0:T(8,128)} async-done(((f32[80,6144]{1,0:T(8,128)}), f32[640,6144]{1,0:T(8,128)}) %all-gather.56.cloned.1.call-update) | async-done | bytes 15728656 | tf_op jit(solution)/shard_map/all_gather | solution.py:344
  1564.2 16.4 write_vector.12.kry_ref
  1580.6 42.9 %all-gather.54.cloned.1.call-done.rows_ref = f32[640,4096]{1,0:T(8,128)} async-done(((f32[80,4096]{1,0:T(8,128)}), f32[640,4096]{1,0:T(8,128)}) %all-gather.54.cloned.1.call-update) | async-done | bytes 10485776 | tf_op jit(solution)/shard_map/all_gather | solution.py:345
  (111 shorter events, 160.8 us)
Async XLA Ops:
  7.2 162.5 %all-gather.22.cloned.1.call-start = ((), (), s32[]{:S(2)}) async-start(), calls=%async_computation.2 | async-start | bytes 17694720 | tf_op jit(solution)/shard_map/all_gather | solution.py:305
  24.3 259.9 %all-gather.20.cloned.1.call-start = ((), (), s32[]{:S(2)}) async-start(), calls=%async_computation.1 | async-start | bytes 26542080 | tf_op jit(solution)/shard_map/all_gather | solution.py:305
  36.1 124.1 %all-to-all-start = ((bf16[6,640,640]{2,0,1:T(8,128)(2,1)}), bf16[6,640,640]{2,0,1:T(8,128)(2,1)}, u32[]{:S(2)}, u32[]{:S(2)}) async-start(bf16[6,640,640]{2,0,1:T(8,128)(2,1)} %copy.18), calls=%async_computation | async-start | bytes 13107200 | tf_op jit(solution)/shard_map/all_to_all | solution.py:306
  39.6 393.9 %all-gather.24.cloned.1.call-start = ((), (), s32[]{:S(2)}) async-start(), calls=%async_computation.3 | async-start | bytes 5898240 | tf_op jit(solution)/shard_map/all_gather | solution.py:331
  284.3 97.2 %copy-start = (f32[80,10240]{1,0:T(8,128)S(1)}, f32[80,10240]{1,0:T(8,128)}, u32[]{:S(2)}) copy-start(f32[80,10240]{1,0:T(8,128)} %get-tuple-element.72.cur_ref.prev_ref) | copy-start | bytes 9830404
  381.4 1.9 copy-start.1
  396.4 1.0 copy-start.7
  397.4 0.8 copy-start.9
  398.2 102.3 %all-gather.26.cloned.1.call-start = ((), (), s32[]{:S(2)}) async-start(), calls=%async_computation.4 | async-start | bytes 8847360 | tf_op jit(solution)/shard_map/all_gather | solution.py:338
  433.6 181.9 %all-gather.28.cloned.1.call-start = ((), (), s32[]{:S(2)}) async-start(), calls=%async_computation.5 | async-start | bytes 29491200 | tf_op jit(solution)/shard_map/all_gather | solution.py:339
  434.2 216.7 %all-gather.30.cloned.1.call-start = ((), (), s32[]{:S(2)}) async-start(), calls=%async_computation.6 | async-start | bytes 5898240 | tf_op jit(solution)/shard_map/all_gather | solution.py:331
  597.5 1.9 copy-start.3
  614.7 0.8 copy-start.8
  615.6 102.4 %all-gather.32.cloned.1.call-start = ((), (), s32[]{:S(2)}) async-start(), calls=%async_computation.7 | async-start | bytes 8847360 | tf_op jit(solution)/shard_map/all_gather | solution.py:338
  651.0 182.0 %all-gather.34.cloned.1.call-start = ((), (), s32[]{:S(2)}) async-start(), calls=%async_computation.8 | async-start | bytes 29491200 | tf_op jit(solution)/shard_map/all_gather | solution.py:339
  651.7 216.7 %all-gather.36.cloned.1.call-start = ((), (), s32[]{:S(2)}) async-start(), calls=%async_computation.9 | async-start | bytes 5898240 | tf_op jit(solution)/shard_map/all_gather | solution.py:331
  814.5 1.9 copy-start.4
  832.9 199.3 %copy-start.10 = (f32[8,128]{1,0:T(8,128)}, f32[8,128]{1,0:T(8,128)S(1)}, u32[]{:S(2)}) copy-start(f32[8,128]{1,0:T(8,128)S(1)} %get-tuple-element.100.bprev_ref) | copy-start | bytes 12292
  833.0 102.6 %all-gather.38.cloned.1.call-start = ((), (), s32[]{:S(2)}) async-start(), calls=%async_computation.10 | async-start | bytes 8847360 | tf_op jit(solution)/shard_map/all_gather | solution.py:338
  868.4 182.3 %all-gather.40.cloned.1.call-start = ((), (), s32[]{:S(2)}) async-start(), calls=%async_computation.11 | async-start | bytes 29491200 | tf_op jit(solution)/shard_map/all_gather | solution.py:339
  869.1 216.9 %all-gather.42.cloned.1.call-start = ((), (), s32[]{:S(2)}) async-start(), calls=%async_computation.12 | async-start | bytes 5898240 | tf_op jit(solution)/shard_map/all_gather | solution.py:331
  1032.2 1.9 copy-start.5
  1050.6 198.7 %copy-start.11 = (f32[8,128]{1,0:T(8,128)}, f32[8,128]{1,0:T(8,128)S(1)}, u32[]{:S(2)}) copy-start(f32[8,128]{1,0:T(8,128)S(1)} %get-tuple-element.111.bprev_ref) | copy-start | bytes 12292
  1050.7 102.1 %all-gather.44.cloned.1.call-start = ((), (), s32[]{:S(2)}) async-start(), calls=%async_computation.13 | async-start | bytes 8847360 | tf_op jit(solution)/shard_map/all_gather | solution.py:338
  1086.1 181.7 %all-gather.46.cloned.1.call-start = ((), (), s32[]{:S(2)}) async-start(), calls=%async_computation.14 | async-start | bytes 29491200 | tf_op jit(solution)/shard_map/all_gather | solution.py:339
  1086.7 216.5 %all-gather.48.cloned.1.call-start = ((), (), s32[]{:S(2)}) async-start(), calls=%async_computation.15 | async-start | bytes 5898240 | tf_op jit(solution)/shard_map/all_gather | solution.py:331
  1249.4 1.9 copy-start.6
  1267.8 102.5 %all-gather.50.cloned.1.call-start = ((), (), s32[]{:S(2)}) async-start(), calls=%async_computation.16 | async-start | bytes 8847360 | tf_op jit(solution)/shard_map/all_gather | solution.py:338
  1303.2 179.7 %all-gather.52.cloned.1.call-start = ((), (), s32[]{:S(2)}) async-start(), calls=%async_computation.17 | async-start | bytes 29491200 | tf_op jit(solution)/shard_map/all_gather | solution.py:339
  1303.8 260.5 %all-gather.56.cloned.1.call-start = ((), (), s32[]{:S(2)}) async-start(), calls=%async_computation.19 | async-start | bytes 17694720 | tf_op jit(solution)/shard_map/all_gather | solution.py:344
  1466.8 1.9 copy-start.2
  1484.4 139.1 %all-gather.54.cloned.1.call-start = ((), (), s32[]{:S(2)}) async-start(), calls=%async_computation.18 | async-start | bytes 11796480 | tf_op jit(solution)/shard_map/all_gather | solution.py:345
Sparse Core Ops, SparseCore 0:
  24.4 145.1 all-gather.21
  171.4 112.7 all-gather.19
  398.3 35.2 all-gather.23
  435.2 46.1 all-gather.25
  483.1 124.0 all-gather.27
  615.7 35.1 all-gather.29
  652.7 46.1 all-gather.31
  700.7 124.0 all-gather.33
  833.1 35.1 all-gather.35
  870.0 46.1 all-gather.37
  918.0 124.0 all-gather.39
  1050.8 35.1 all-gather.41
  1087.9 46.1 all-gather.43
  1135.7 124.0 all-gather.45
  1267.9 35.2 all-gather.47
  1304.8 46.1 all-gather.49
  1352.7 124.0 all-gather.51
  1484.5 79.6 all-gather.55
  1566.0 57.3 all-gather.53

commit v2 on v1

--- a/solution.py
+++ b/solution.py
@@ -11,12 +11,13 @@
 LANE = 128
 SUB = 16
 GROUP = 6
-PIECES = (2, 3)
+PIECES = ((2,), (2, 1))
 MESH = pl.DeviceIdType.MESH
 
 
-def ham_kernel(bond, pair, slab, group, first, u_ref, r_ref, w_ref, l_ref, *rest):
+def ham_kernel(bond, pair, slab, group, first, u_ref, r_ref, w_ref, *rest):
     out_ref, y1, y2 = rest[-3:]
+    l_refs = rest[:-3] if first else rest[:-4]
     inner = u_ref.shape[1] // (pair * LANE)
     chunks = bond // LANE
     bgroups = slab // SUB
@@ -24,7 +25,7 @@
 
     @pl.when(pl.program_id(0) == 0)
     def _():
-        out_ref[...] = jnp.zeros_like(out_ref) if first else rest[0][...]
+        out_ref[...] = jnp.zeros_like(out_ref) if first else rest[-4][...]
 
     def right(i, _):
         cols = pl.ds(pl.multiple_of(i * width, width), width)
@@ -33,6 +34,11 @@
 
     lax.fori_loop(0, inner, right, 0, unroll=True)
 
+    parts = []
+    for l_ref in l_refs:
+        size = l_ref.shape[0] // (group * LANE)
+        parts.append((sum(n for _, n in parts), size))
+    place = {lo + n: (lo * group + n, size) for lo, size in parts for n in range(size)}
     blocks = [(bg, ac) for bg in range(bgroups) for ac in range(inner)]
 
     def site(k, _):
@@ -47,7 +53,8 @@
             rhs = tiles[0] if len(tiles) == 1 else jnp.concatenate(tiles, axis=1)
             res = jnp.dot(w_k, rhs, preferred_element_type=jnp.float32).astype(jnp.bfloat16)
             for n, (bg, ac) in enumerate(part):
-                cols = pl.ds(pl.multiple_of((k * inner + ac) * LANE, LANE), LANE)
+                lead, size = place[ac]
+                cols = pl.ds(pl.multiple_of((lead + k * size) * LANE, LANE), LANE)
                 for q in range(pair):
                     y2[q * slab + bg * SUB : q * slab + (bg + 1) * SUB, cols] = res[q * SUB : (q + 1) * SUB, n * LANE : (n + 1) * LANE]
         return 0
@@ -58,7 +65,9 @@
 
     def left(i, _):
         sub = pl.ds(pl.multiple_of(i * (qs * slab), qs * slab), qs * slab)
-        res = jnp.dot(y2[sub, :], l_ref[...], preferred_element_type=jnp.float32)
+        res = 0.0
+        for l_ref, (lo, size) in zip(l_refs, parts):
+            res += jnp.dot(y2[sub, lo * group * LANE : (lo + size) * group * LANE], l_ref[...], preferred_element_type=jnp.float32)
         for ac in range(chunks):
             for n in range(qs):
                 cols = pl.ds(pl.multiple_of((ac * pair + n) * LANE + i * (qs * LANE), LANE), LANE)
@@ -84,8 +93,7 @@
             pl.BlockSpec((bond, span * pair), full, pipeline_mode=pl.Buffered(1)),
             pl.BlockSpec((GROUP * slab, bond), lambda i: (i, 0)),
             pl.BlockSpec((GROUP, side, side), lambda i: (i, 0, 0)),
-            pl.BlockSpec((GROUP * span, bond), lambda i: (i, 0)),
-        ] + ([] if first else [once]),
+        ] + [pl.BlockSpec((GROUP * rows.shape[0] // terms, bond), lambda i: (i, 0)) for rows in left_rows] + ([] if first else [once]),
         out_specs=once,
         out_shape=jax.ShapeDtypeStruct((slab, bond * pair), jnp.float32),
         scratch_shapes=[
@@ -95,7 +103,7 @@
         compiler_params=pltpu.CompilerParams(dimension_semantics=("arbitrary",), vmem_limit_bytes=60_000_000),
         cost_estimate=pl.CostEstimate(flops=flops, bytes_accessed=50_000_000, transcendentals=0),
         name="apply_ham",
-    )(u_part, right_rows, site_kron, left_rows, *([] if first else [sigma]))
+    )(u_part, right_rows, site_kron, *left_rows, *([] if first else [sigma]))
 
 
 def update_kernel(devices, sig_ref, cur_ref, prev_ref, bprev_ref, nxt_ref, alpha_ref, beta_ref, *rest):
@@ -297,12 +305,17 @@
         chunks = bond // LANE
         row_start = lax.axis_index("terms") * slab
 
-        bounds = [sum(PIECES[:n]) * LANE for n in range(len(PIECES) + 1)]
-        spans = list(zip(bounds[:-1], bounds[1:]))
+        def ranges(sizes):
+            ends = [sum(sizes[: n + 1]) * LANE for n in range(len(sizes))]
+            return list(zip([0] + ends[:-1], ends))
+
+        fine = ranges([n for piece in PIECES for n in piece])
+        spans = ranges([sum(piece) for piece in PIECES])
         widths = [(hi - lo) * pair for lo, hi in spans]
         site_all = lax.all_gather(site_loc, "terms", axis=0, tiled=True)
         left_loc, site_all = lax.optimization_barrier((left_loc, site_all))
-        lefts = [lax.all_gather(left_loc[:, lo:hi], "terms", axis=0, tiled=True).reshape(-1, bond) for lo, hi in spans]
+        singles = [[lax.all_gather(left_loc[:, lo:hi], "terms", axis=0, tiled=True).reshape(-1, bond)] for lo, hi in fine]
+        lefts = [[rows[0] for rows, (start, _) in zip(singles, fine) if lo <= start < hi] for lo, hi in spans]
         right_rows = lax.all_to_all(right_loc, "terms", 1, 0, tiled=True).reshape(-1, bond)
         eye = jnp.eye(SUB, dtype=jnp.bfloat16)
         site_kron = (site_all[:, :, None, :, None] * eye[None, None, :, None, :]).reshape(-1, pair * SUB, pair * SUB)
@@ -311,14 +324,14 @@
         krylov, u_full, cur = start_vectors(psi, norm, LANCZOS_STEPS + 1, slab)
         prev = jnp.zeros_like(cur)
         beta = jnp.zeros((8, LANE), jnp.float32)
-        us = [u_full[:, lo * pair : hi * pair] for lo, hi in spans]
+        us = [u_full[:, lo * pair : hi * pair] for lo, hi in fine]
         full = None
         alphas = []
         betas = []
         for step_idx in range(LANCZOS_STEPS):
             last = step_idx == LANCZOS_STEPS - 1
             sigma = None
-            for u_part, left_rows in zip(us, lefts):
+            for u_part, left_rows in zip(us, lefts if step_idx else singles):
                 sigma = apply_ham(u_part, right_rows, site_kron, left_rows, sigma, pair, slab)
             nxt, alpha, beta, *lows = update(groups, () if last else widths, sigma, cur, prev, beta)
             late = nxt

time: 1650 us -> 1630 us (0.988)
  waiting for transfers between devices: 240 us -> 210 us
    all_gather x2 -> x3, waiting for transfers between devices: 52.2 us -> 18.9 us  [body(): lax.all_gather(left_loc[:, lo:hi], 'terms', axis=0, tiled=True)]
    pallas_call x12 -> x13, Pallas kernels: 978 us -> 987 us  [apply_ham(): pl.pallas_call(functools.partial(ham_kernel, bond, pair, slab, GROUP, fir...]
  transfers between devices with their start and end apart: 20 -> 21, of which waited for: 10 -> 10; matrix products, arithmetic and copies ran while one was open for 6% -> 6% of each run, Pallas kernels for 69% -> 74%
where the time goes in v2:
time: 1630 us; the launch traced here: 1620 us
  Pallas kernels  1260 us (77%)
  waiting for transfers between devices  210 us (13%)
  local copies, waits for them, and re-layouts  93.9 us (6%)
  other arithmetic  19.2 us (1%)
    pallas_call x13, Pallas kernels, apply_ham(): pl.pallas_call(functools.partial(ham_kernel, bond, pair, slab, GROUP, fir...  987 us
    pallas_call x7, Pallas kernels, write_vector(): pl.pallas_call(functools.partial(out_kernel, phys), grid=(rows.shape[1] /...  150 us
    pallas_call x6, Pallas kernels, update(): pl.pallas_call(functools.partial(update_kernel, devices), out_shape=[jax....  91.7 us
    all_gather x5, waiting for transfers between devices, body(): us = [lax.all_gather(lows[0], 'terms', axis=0, tiled=True)]  79.1 us
    all_gather x1, waiting for transfers between devices, body(): tail = lax.all_gather(late[:, cut:], 'terms', axis=0, tiled=True)  42.7 us
    all_gather x1, waiting for transfers between devices, body(): head = lax.all_gather(late[:, :cut], 'terms', axis=0, tiled=True)  38 us
    pallas_call x1, Pallas kernels, start_vectors(): pl.pallas_call(functools.partial(start_kernel, phys, slab), grid=(bond //...  34.9 us
  transfers between devices with their start and end apart: 21, of which 10 were waited for; matrix products, arithmetic and copies ran while one was open for 6% of the time, Pallas kernels for 74%

profile of v2, /device:TPU:0, one launch (start us, length us, event | category | flops | bytes accessed | tf_op | source)
XLA Modules:
  0.0 1621.2 jit_solution(13776082841807057304)
XLA Ops:
  41.0 15.9 multiply_reduce_fusion
  65.4 17.4 %copy.21 = bf16[48,256,256]{2,1,0:T(8,128)(2,1)} copy(bf16[48,256,256]{0,2,1:T(8,128)(2,1)} %bitcast.22) | data formatting | bytes 12582912 | tf_op jit(solution)/shard_map/mul | solution.py:321
  82.8 34.9 %start_vectors.1 = (f32[7,640,4,4,640]{4,3,2,1,0:T(4,128)}, bf16[640,10240]{1,0:T(8,128)(2,1)}, f32[80,10240]{1,0:T(8,128)}) custom-call(f32[640,4,4,640]{3,2,1,0:T(4,128)} %psi_ref.1, f32[1,128]{1,0:T(1,128)S(1)} %broadcast_in_dim.11.norm_ref), custom_call_target="tpu_custom_call" | custom-call | flops 60000000 | bytes 70000000 | tf_op jit(solution)/shard_map/start_vectors/pallas_call | solution.py:277
  134.1 27.2 %all-to-all-done = bf16[6,640,640]{2,0,1:T(8,128)(2,1)} async-done(((bf16[6,640,640]{2,0,1:T(8,128)(2,1)}), bf16[6,640,640]{2,0,1:T(8,128)(2,1)}, u32[]{:S(2)}, u32[]{:S(2)}) %all-to-all-start) | async-done | bytes 4915232 | tf_op jit(solution)/shard_map/all_to_all | solution.py:319
  171.2 66.4 %apply_ham.13.rest_1_ = f32[80,10240]{1,0:T(8,128)} custom-call(bf16[640,4096]{1,0:T(8,128)(2,1)} %get-tuple-element.135.u_ref, bf16[3840,640]{1,0:T(8,128)(2,1)} %bitcast.23, bf16[48,256,256]{2,1,0:T(8,128)(2,1)} %broadcast_multiply_fusion.w_ref, bf16[12288,640]{1,0:T(8,128)(2,1)} %bitcast.36), custom_call_target="tpu_custom_call" | custom-call | flops 48318382080 | bytes 50000000 | tf_op jit(solution)/shard_map/apply_ham/pallas_call | solution.py:89
  237.6 14.8 all-gather.23.cloned.1.call-done
  252.5 66.9 %apply_ham.14.rest_1_ = f32[80,10240]{1,0:T(8,128)} custom-call(bf16[640,4096]{1,0:T(8,128)(2,1)} %get-tuple-element.136.u_ref, bf16[3840,640]{1,0:T(8,128)(2,1)} %bitcast.24, bf16[48,256,256]{2,1,0:T(8,128)(2,1)} %broadcast_multiply_fusion.w_ref, bf16[12288,640]{1,0:T(8,128)(2,1)} %bitcast.42, f32[80,10240]{1,0:T(8,128)} %apply_ham.13.rest_1_), custom_call_target="tpu_custom_call" | custom-call | flops 48318382080 | bytes 50000000 | tf_op jit(solution)/shard_map/apply_ham/pallas_call | solution.py:89
  319.3 37.8 %apply_ham.15.sig_ref = f32[80,10240]{1,0:T(8,128)} custom-call(bf16[640,2048]{1,0:T(8,128)(2,1)} %slice.60.u_ref, bf16[3840,640]{1,0:T(8,128)(2,1)} %bitcast.25, bf16[48,256,256]{2,1,0:T(8,128)(2,1)} %broadcast_multiply_fusion.w_ref, bf16[6144,640]{1,0:T(8,128)(2,1)} %bitcast.48, f32[80,10240]{1,0:T(8,128)} %apply_ham.14.rest_1_), custom_call_target="tpu_custom_call" | custom-call | flops 24159191040 | bytes 50000000 | tf_op jit(solution)/shard_map/apply_ham/pallas_call | solution.py:89
  375.8 35.3 %all-gather.27.cloned.1.call-done.u_ref = bf16[640,4096]{1,0:T(8,128)(2,1)} async-done(((bf16[80,4096]{1,0:T(8,128)(2,1)}), bf16[640,4096]{1,0:T(8,128)(2,1)}) %all-gather.27.cloned.1.call-update) | async-done | bytes 5242896 | tf_op jit(solution)/shard_map/all_gather | solution.py:344
  411.8 66.1 %apply_ham.16.rest_2_ = f32[80,10240]{1,0:T(8,128)} custom-call(bf16[640,4096]{1,0:T(8,128)(2,1)} %all-gather.27.cloned.1.call-done.u_ref, bf16[3840,640]{1,0:T(8,128)(2,1)} %bitcast.26, bf16[48,256,256]{2,1,0:T(8,128)(2,1)} %broadcast_multiply_fusion.w_ref, bf16[12288,640]{1,0:T(8,128)(2,1)} %bitcast.37), custom_call_target="tpu_custom_call" | custom-call | flops 48318382080 | bytes 50000000 | tf_op jit(solution)/shard_map/apply_ham/pallas_call | solution.py:89
  477.9 97.3 %apply_ham.17.sig_ref = f32[80,10240]{1,0:T(8,128)} custom-call(bf16[640,6144]{1,0:T(8,128)(2,1)} %all-gather.29.cloned.1.call-done.u_ref, bf16[3840,640]{1,0:T(8,128)(2,1)} %bitcast.27, bf16[48,256,256]{2,1,0:T(8,128)(2,1)} %broadcast_multiply_fusion.w_ref, bf16[12288,640]{1,0:T(8,128)(2,1)} %bitcast.43, bf16[6144,640]{1,0:T(8,128)(2,1)} %bitcast.49, ...), custom_call_target="tpu_custom_call" | custom-call | flops 72477573120 | bytes 50000000 | tf_op jit(solution)/shard_map/apply_ham/pallas_call | solution.py:89
  577.1 15.2 lanczos_update.7
  593.2 24.4 %write_vector.7.kry_ref = f32[7,640,4,4,640]{4,3,2,1,0:T(4,128)} custom-call(f32[640,10240]{1,0:T(8,128)} %all-gather.31.cloned.1.call-done.rows_ref, f32[7,640,4,4,640]{4,3,2,1,0:T(4,128)} %get-tuple-element.82.kry_ref), custom_call_target="tpu_custom_call", output_to_operand_aliasing={{}: (1, {})} | custom-call | flops 30000000 | bytes 54000000 | tf_op jit(solution)/shard_map/write_vector/pallas_call | solution.py:234
  629.4 66.3 %apply_ham.18.rest_2_ = f32[80,10240]{1,0:T(8,128)} custom-call(bf16[640,4096]{1,0:T(8,128)(2,1)} %all-gather.33.cloned.1.call-done.u_ref, bf16[3840,640]{1,0:T(8,128)(2,1)} %bitcast.28, bf16[48,256,256]{2,1,0:T(8,128)(2,1)} %broadcast_multiply_fusion.w_ref, bf16[12288,640]{1,0:T(8,128)(2,1)} %bitcast.38), custom_call_target="tpu_custom_call" | custom-call | flops 48318382080 | bytes 50000000 | tf_op jit(solution)/shard_map/apply_ham/pallas_call | solution.py:89
  695.7 96.9 %apply_ham.19.sig_ref = f32[80,10240]{1,0:T(8,128)} custom-call(bf16[640,6144]{1,0:T(8,128)(2,1)} %all-gather.35.cloned.1.call-done.u_ref, bf16[3840,640]{1,0:T(8,128)(2,1)} %bitcast.29, bf16[48,256,256]{2,1,0:T(8,128)(2,1)} %broadcast_multiply_fusion.w_ref, bf16[12288,640]{1,0:T(8,128)(2,1)} %bitcast.44, bf16[6144,640]{1,0:T(8,128)(2,1)} %bitcast.50, ...), custom_call_target="tpu_custom_call" | custom-call | flops 72477573120 | bytes 50000000 | tf_op jit(solution)/shard_map/apply_ham/pallas_call | solution.py:89
  794.5 16.6 %lanczos_update.8 = (f32[80,10240]{1,0:T(8,128)}, f32[8,128]{1,0:T(8,128)S(1)}, f32[8,128]{1,0:T(8,128)S(1)}, bf16[80,4096]{1,0:T(8,128)(2,1)}, bf16[80,6144]{1,0:T(8,128)(2,1)}) custom-call(f32[80,10240]{1,0:T(8,128)S(1)} %copy-done.4, f32[80,10240]{1,0:T(8,128)} %get-tuple-element.91.cur_ref.prev_ref, f32[80,10240]{1,0:T(8,128)} %get-tuple-element.80.cur_ref.prev_ref, ...), custom_call_target="tpu_custom_call" | custom-call | flops 20000000 | bytes 20000000 | tf_op jit(solution)/shard_map/lanczos_update/pallas_call | solution.py:191
  811.2 24.4 %write_vector.8.kry_ref = f32[7,640,4,4,640]{4,3,2,1,0:T(4,128)} custom-call(f32[640,10240]{1,0:T(8,128)} %all-gather.37.cloned.1.call-done.rows_ref, f32[7,640,4,4,640]{4,3,2,1,0:T(4,128)} %write_vector.7.kry_ref), custom_call_target="tpu_custom_call", output_to_operand_aliasing={{}: (1, {})} | custom-call | flops 30000000 | bytes 54000000 | tf_op jit(solution)/shard_map/write_vector/pallas_call | solution.py:234
  847.2 66.4 %apply_ham.20.rest_2_ = f32[80,10240]{1,0:T(8,128)} custom-call(bf16[640,4096]{1,0:T(8,128)(2,1)} %all-gather.39.cloned.1.call-done.u_ref, bf16[3840,640]{1,0:T(8,128)(2,1)} %bitcast.30, bf16[48,256,256]{2,1,0:T(8,128)(2,1)} %broadcast_multiply_fusion.w_ref, bf16[12288,640]{1,0:T(8,128)(2,1)} %bitcast.39), custom_call_target="tpu_custom_call" | custom-call | flops 48318382080 | bytes 50000000 | tf_op jit(solution)/shard_map/apply_ham/pallas_call | solution.py:89
  913.5 96.9 %apply_ham.21.sig_ref = f32[80,10240]{1,0:T(8,128)} custom-call(bf16[640,6144]{1,0:T(8,128)(2,1)} %all-gather.41.cloned.1.call-done.u_ref, bf16[3840,640]{1,0:T(8,128)(2,1)} %bitcast.31, bf16[48,256,256]{2,1,0:T(8,128)(2,1)} %broadcast_multiply_fusion.w_ref, bf16[12288,640]{1,0:T(8,128)(2,1)} %bitcast.45, bf16[6144,640]{1,0:T(8,128)(2,1)} %bitcast.51, ...), custom_call_target="tpu_custom_call" | custom-call | flops 72477573120 | bytes 50000000 | tf_op jit(solution)/shard_map/apply_ham/pallas_call | solution.py:89
  1012.3 16.4 %lanczos_update.9 = (f32[80,10240]{1,0:T(8,128)}, f32[8,128]{1,0:T(8,128)S(1)}, f32[8,128]{1,0:T(8,128)S(1)}, bf16[80,4096]{1,0:T(8,128)(2,1)}, bf16[80,6144]{1,0:T(8,128)(2,1)}) custom-call(f32[80,10240]{1,0:T(8,128)S(1)} %copy-done.5, f32[80,10240]{1,0:T(8,128)} %get-tuple-element.102.cur_ref.prev_ref, f32[80,10240]{1,0:T(8,128)} %get-tuple-element.91.cur_ref.prev_ref, ...), custom_call_target="tpu_custom_call" | custom-call | flops 20000000 | bytes 20000000 | tf_op jit(solution)/shard_map/lanczos_update/pallas_call | solution.py:191
  1028.9 24.4 %write_vector.9.kry_ref = f32[7,640,4,4,640]{4,3,2,1,0:T(4,128)} custom-call(f32[640,10240]{1,0:T(8,128)} %all-gather.43.cloned.1.call-done.rows_ref, f32[7,640,4,4,640]{4,3,2,1,0:T(4,128)} %write_vector.8.kry_ref), custom_call_target="tpu_custom_call", output_to_operand_aliasing={{}: (1, {})} | custom-call | flops 30000000 | bytes 54000000 | tf_op jit(solution)/shard_map/write_vector/pallas_call | solution.py:234
  1064.9 66.1 %apply_ham.22.rest_2_ = f32[80,10240]{1,0:T(8,128)} custom-call(bf16[640,4096]{1,0:T(8,128)(2,1)} %all-gather.45.cloned.1.call-done.u_ref, bf16[3840,640]{1,0:T(8,128)(2,1)} %bitcast.32, bf16[48,256,256]{2,1,0:T(8,128)(2,1)} %broadcast_multiply_fusion.w_ref, bf16[12288,640]{1,0:T(8,128)(2,1)} %bitcast.40), custom_call_target="tpu_custom_call" | custom-call | flops 48318382080 | bytes 50000000 | tf_op jit(solution)/shard_map/apply_ham/pallas_call | solution.py:89
  1131.0 96.9 %apply_ham.23.sig_ref = f32[80,10240]{1,0:T(8,128)} custom-call(bf16[640,6144]{1,0:T(8,128)(2,1)} %all-gather.47.cloned.1.call-done.u_ref, bf16[3840,640]{1,0:T(8,128)(2,1)} %bitcast.33, bf16[48,256,256]{2,1,0:T(8,128)(2,1)} %broadcast_multiply_fusion.w_ref, bf16[12288,640]{1,0:T(8,128)(2,1)} %bitcast.46, bf16[6144,640]{1,0:T(8,128)(2,1)} %bitcast.52, ...), custom_call_target="tpu_custom_call" | custom-call | flops 72477573120 | bytes 50000000 | tf_op jit(solution)/shard_map/apply_ham/pallas_call | solution.py:89
  1229.8 16.4 %lanczos_update.10 = (f32[80,10240]{1,0:T(8,128)}, f32[8,128]{1,0:T(8,128)S(1)}, f32[8,128]{1,0:T(8,128)S(1)}, bf16[80,4096]{1,0:T(8,128)(2,1)}, bf16[80,6144]{1,0:T(8,128)(2,1)}) custom-call(f32[80,10240]{1,0:T(8,128)S(1)} %copy-done.6, f32[80,10240]{1,0:T(8,128)} %get-tuple-element.113.cur_ref.prev_ref, f32[80,10240]{1,0:T(8,128)} %get-tuple-element.102.cur_ref.prev_ref, ...), custom_call_target="tpu_custom_call" | custom-call | flops 20000000 | bytes 20000000 | tf_op jit(solution)/shard_map/lanczos_update/pallas_call | solution.py:191
  1246.3 24.4 %write_vector.10.kry_ref = f32[7,640,4,4,640]{4,3,2,1,0:T(4,128)} custom-call(f32[640,10240]{1,0:T(8,128)} %all-gather.49.cloned.1.call-done.rows_ref, f32[7,640,4,4,640]{4,3,2,1,0:T(4,128)} %write_vector.9.kry_ref), custom_call_target="tpu_custom_call", output_to_operand_aliasing={{}: (1, {})} | custom-call | flops 30000000 | bytes 54000000 | tf_op jit(solution)/shard_map/write_vector/pallas_call | solution.py:234
  1282.3 66.5 %apply_ham.24.rest_2_ = f32[80,10240]{1,0:T(8,128)} custom-call(bf16[640,4096]{1,0:T(8,128)(2,1)} %all-gather.51.cloned.1.call-done.u_ref, bf16[3840,640]{1,0:T(8,128)(2,1)} %bitcast.34, bf16[48,256,256]{2,1,0:T(8,128)(2,1)} %broadcast_multiply_fusion.w_ref, bf16[12288,640]{1,0:T(8,128)(2,1)} %bitcast.41), custom_call_target="tpu_custom_call" | custom-call | flops 48318382080 | bytes 50000000 | tf_op jit(solution)/shard_map/apply_ham/pallas_call | solution.py:89
  1348.8 96.9 %apply_ham.25.sig_ref = f32[80,10240]{1,0:T(8,128)} custom-call(bf16[640,6144]{1,0:T(8,128)(2,1)} %all-gather.53.cloned.1.call-done.u_ref, bf16[3840,640]{1,0:T(8,128)(2,1)} %bitcast.35, bf16[48,256,256]{2,1,0:T(8,128)(2,1)} %broadcast_multiply_fusion.w_ref, bf16[12288,640]{1,0:T(8,128)(2,1)} %bitcast.47, bf16[6144,640]{1,0:T(8,128)(2,1)} %bitcast.53, ...), custom_call_target="tpu_custom_call" | custom-call | flops 72477573120 | bytes 50000000 | tf_op jit(solution)/shard_map/apply_ham/pallas_call | solution.py:89
  1447.6 14.1 lanczos_update.11
  1480.6 24.5 %write_vector.11.kry_ref = f32[7,640,4,4,640]{4,3,2,1,0:T(4,128)} custom-call(f32[640,10240]{1,0:T(8,128)} %all-gather.55.cloned.1.call-done.rows_ref, f32[7,640,4,4,640]{4,3,2,1,0:T(4,128)} %write_vector.10.kry_ref), custom_call_target="tpu_custom_call", output_to_operand_aliasing={{}: (1, {})} | custom-call | flops 30000000 | bytes 54000000 | tf_op jit(solution)/shard_map/write_vector/pallas_call | solution.py:234
  1505.1 38.0 %all-gather.59.cloned.1.call-done.rows_ref = f32[640,6144]{1,0:T(8,128)} async-done(((f32[80,6144]{1,0:T(8,128)}), f32[640,6144]{1,0:T(8,128)}) %all-gather.59.cloned.1.call-update) | async-done | bytes 15728656 | tf_op jit(solution)/shard_map/all_gather | solution.py:357
  1543.1 16.4 %write_vector.12.kry_ref = f32[7,640,4,4,640]{4,3,2,1,0:T(4,128)} custom-call(f32[640,6144]{1,0:T(8,128)} %all-gather.59.cloned.1.call-done.rows_ref, f32[7,640,4,4,640]{4,3,2,1,0:T(4,128)} %write_vector.11.kry_ref), custom_call_target="tpu_custom_call", output_to_operand_aliasing={{}: (1, {})} | custom-call | flops 30000000 | bytes 54000000 | tf_op jit(solution)/shard_map/write_vector/pallas_call | solution.py:234
  1559.5 42.7 %all-gather.57.cloned.1.call-done.rows_ref = f32[640,4096]{1,0:T(8,128)} async-done(((f32[80,4096]{1,0:T(8,128)}), f32[640,4096]{1,0:T(8,128)}) %all-gather.57.cloned.1.call-update) | async-done | bytes 10485776 | tf_op jit(solution)/shard_map/all_gather | solution.py:358
  (117 shorter events, 174.9 us)
Async XLA Ops:
  7.2 164.0 %all-gather.25.cloned.1.call-start = ((), (), s32[]{:S(2)}) async-start(), calls=%async_computation.3 | async-start | bytes 17694720 | tf_op jit(solution)/shard_map/all_gather | solution.py:317
  25.9 226.6 %all-gather.23.cloned.1.call-start = ((), (), s32[]{:S(2)}) async-start(), calls=%async_computation.2 | async-start | bytes 17694720 | tf_op jit(solution)/shard_map/all_gather | solution.py:317
  26.6 292.7 %all-gather.21.cloned.1.call-start = ((), (), s32[]{:S(2)}) async-start(), calls=%async_computation.1 | async-start | bytes 8847360 | tf_op jit(solution)/shard_map/all_gather | solution.py:317
  37.1 124.3 %all-to-all-start = ((bf16[6,640,640]{2,0,1:T(8,128)(2,1)}), bf16[6,640,640]{2,0,1:T(8,128)(2,1)}, u32[]{:S(2)}, u32[]{:S(2)}) async-start(bf16[6,640,640]{2,0,1:T(8,128)(2,1)} %copy.18), calls=%async_computation | async-start | bytes 13107200 | tf_op jit(solution)/shard_map/all_to_all | solution.py:319
  40.6 370.5 %all-gather.27.cloned.1.call-start = ((), (), s32[]{:S(2)}) async-start(), calls=%async_computation.4 | async-start | bytes 5898240 | tf_op jit(solution)/shard_map/all_gather | solution.py:344
  82.8 38.5 %copy-start.12 = (bf16[48,256,256]{2,1,0:T(8,128)(2,1)S(1)}, bf16[48,256,256]{2,1,0:T(8,128)(2,1)}, u32[]{:S(2)}) copy-start(bf16[48,256,256]{2,1,0:T(8,128)(2,1)} %copy.21) | copy-start | bytes 18874372
  357.2 1.9 copy-start
  359.1 1.9 copy-start.1
  374.0 0.9 copy-start.7
  375.8 102.2 %all-gather.29.cloned.1.call-start = ((), (), s32[]{:S(2)}) async-start(), calls=%async_computation.5 | async-start | bytes 8847360 | tf_op jit(solution)/shard_map/all_gather | solution.py:351
  411.2 182.0 %all-gather.31.cloned.1.call-start = ((), (), s32[]{:S(2)}) async-start(), calls=%async_computation.6 | async-start | bytes 29491200 | tf_op jit(solution)/shard_map/all_gather | solution.py:352
  411.7 216.8 %all-gather.33.cloned.1.call-start = ((), (), s32[]{:S(2)}) async-start(), calls=%async_computation.7 | async-start | bytes 5898240 | tf_op jit(solution)/shard_map/all_gather | solution.py:344
  575.2 1.9 copy-start.3
  593.2 102.5 %all-gather.35.cloned.1.call-start = ((), (), s32[]{:S(2)}) async-start(), calls=%async_computation.8 | async-start | bytes 8847360 | tf_op jit(solution)/shard_map/all_gather | solution.py:351
  628.6 182.5 %all-gather.37.cloned.1.call-start = ((), (), s32[]{:S(2)}) async-start(), calls=%async_computation.9 | async-start | bytes 29491200 | tf_op jit(solution)/shard_map/all_gather | solution.py:352
  629.3 217.2 %all-gather.39.cloned.1.call-start = ((), (), s32[]{:S(2)}) async-start(), calls=%async_computation.10 | async-start | bytes 5898240 | tf_op jit(solution)/shard_map/all_gather | solution.py:344
  792.6 1.9 copy-start.4
  811.1 199.3 %copy-start.10 = (f32[8,128]{1,0:T(8,128)}, f32[8,128]{1,0:T(8,128)S(1)}, u32[]{:S(2)}) copy-start(f32[8,128]{1,0:T(8,128)S(1)} %get-tuple-element.100.bprev_ref) | copy-start | bytes 12292
  811.1 102.4 %all-gather.41.cloned.1.call-start = ((), (), s32[]{:S(2)}) async-start(), calls=%async_computation.11 | async-start | bytes 8847360 | tf_op jit(solution)/shard_map/all_gather | solution.py:351
  846.5 182.3 %all-gather.43.cloned.1.call-start = ((), (), s32[]{:S(2)}) async-start(), calls=%async_computation.12 | async-start | bytes 29491200 | tf_op jit(solution)/shard_map/all_gather | solution.py:352
  847.1 217.1 %all-gather.45.cloned.1.call-start = ((), (), s32[]{:S(2)}) async-start(), calls=%async_computation.13 | async-start | bytes 5898240 | tf_op jit(solution)/shard_map/all_gather | solution.py:344
  1010.4 1.9 copy-start.5
  1028.8 199.1 %copy-start.11 = (f32[8,128]{1,0:T(8,128)}, f32[8,128]{1,0:T(8,128)S(1)}, u32[]{:S(2)}) copy-start(f32[8,128]{1,0:T(8,128)S(1)} %get-tuple-element.111.bprev_ref) | copy-start | bytes 12292
  1028.8 102.2 %all-gather.47.cloned.1.call-start = ((), (), s32[]{:S(2)}) async-start(), calls=%async_computation.14 | async-start | bytes 8847360 | tf_op jit(solution)/shard_map/all_gather | solution.py:351
  1064.2 182.0 %all-gather.49.cloned.1.call-start = ((), (), s32[]{:S(2)}) async-start(), calls=%async_computation.15 | async-start | bytes 29491200 | tf_op jit(solution)/shard_map/all_gather | solution.py:352
  1064.8 216.8 %all-gather.51.cloned.1.call-start = ((), (), s32[]{:S(2)}) async-start(), calls=%async_computation.16 | async-start | bytes 5898240 | tf_op jit(solution)/shard_map/all_gather | solution.py:344
  1227.9 1.9 copy-start.6
  1246.3 102.6 %all-gather.53.cloned.1.call-start = ((), (), s32[]{:S(2)}) async-start(), calls=%async_computation.17 | async-start | bytes 8847360 | tf_op jit(solution)/shard_map/all_gather | solution.py:351
  1281.7 180.1 %all-gather.55.cloned.1.call-start = ((), (), s32[]{:S(2)}) async-start(), calls=%async_computation.18 | async-start | bytes 29491200 | tf_op jit(solution)/shard_map/all_gather | solution.py:352
  1282.2 260.9 %all-gather.59.cloned.1.call-start = ((), (), s32[]{:S(2)}) async-start(), calls=%async_computation.20 | async-start | bytes 17694720 | tf_op jit(solution)/shard_map/all_gather | solution.py:357
  1445.7 1.9 copy-start.2
  1463.3 138.9 %all-gather.57.cloned.1.call-start = ((), (), s32[]{:S(2)}) async-start(), calls=%async_computation.19 | async-start | bytes 11796480 | tf_op jit(solution)/shard_map/all_gather | solution.py:358
  (2 other events, 1.7 us)
Sparse Core Ops, SparseCore 0:
  26.0 145.1 all-gather.24
  173.0 79.4 all-gather.22
  254.3 46.1 all-gather.20
  375.9 35.2 all-gather.26
  412.8 46.1 all-gather.28
  460.6 124.0 all-gather.30
  593.3 35.2 all-gather.32
  630.4 46.1 all-gather.34
  678.4 124.0 all-gather.36
  811.3 35.1 all-gather.38
  848.3 46.1 all-gather.40
  896.2 124.1 all-gather.42
  1029.0 35.2 all-gather.44
  1065.9 46.1 all-gather.46
  1113.7 124.0 all-gather.48
  1246.4 35.2 all-gather.50
  1283.3 46.1 all-gather.52
  1331.1 124.0 all-gather.54
  1463.4 79.6 all-gather.58
  1544.8 57.3 all-gather.56
